TPU v7x, 128 devices: a whole 4x4x4 slice. The times are simulated.
128 devices in a mesh: dp: 32 (over z, y, core), mp: 4 (over x).
Axes of the slice: x: 4, y: 4, z: 4, core: 2. Of those that a mesh axis runs over, the one named last changes fastest.
Arguments:
- queries: bfloat16 [1024, 64, 128], P('dp', 'mp'), may hold values from -8 to 8
- lookup_sheets: bfloat16 [32768, 16, 8, 128], P('dp', None, 'mp'), may hold values from -6 to 6
- content_sheets: bfloat16 [32768, 16, 8, 128], P('dp', None, 'mp'), may hold values from -12 to 12
- page_table: int32 [1024, 32], replicated, may hold values from 0 to 32767, as said below
- context_len: int32 [1024], replicated, may hold values from 32 to 512, as said below
- out_weight: bfloat16 [8192, 8192], P('mp', 'dp'), may hold values from -0.0625 to 0.0625
Outputs:
- attention: bfloat16 [1024, 64, 128], P('dp', 'mp')
- projected: bfloat16 [1024, 8192], P('mp', 'dp')
Inputs may be any that keep to these rules, and one draw needn't show every extreme that they name: `page_table`: every entry names a pool page, 0 to 32767, and every pool page appears exactly once in the whole table. `context_len`: each length lies between 32 and 512; most contexts are short, and some request has exactly 512 tokens.
All inputs are finite; a program needn't handle non-finite values.
Results may differ from a plain program's by a relative error of at most 0.0015.
Values may be sent and summed in bfloat16 or wider, within the bound.
A program may use at most 128 MiB of HBM per device.

v0:
```python
import functools

import jax
import jax.numpy as jnp
from jax import lax
from jax.experimental import pallas as pl
from jax.experimental.pallas import tpu as pltpu
from jax.sharding import PartitionSpec as P

MESH = pl.DeviceIdType.MESH
NEG = -1e30
DEPTH = 4
PRE = 2
PARTS = 2


def axis_barrier(axes):
    barrier = pltpu.get_barrier_semaphore()
    total = 0
    for name in axes:
        n = lax.axis_size(name)
        me = lax.axis_index(name)
        for step in range(1, n):
            pl.semaphore_signal(
                barrier, inc=1, device_id={name: lax.rem(me + step, n)}, device_id_type=MESH
            )
        total += n - 1
    pl.semaphore_wait(barrier, total)


def line_gather(buf, right_sem, left_sem, side_sem, recv_sem):
    n = lax.axis_size("dp")
    me = lax.axis_index("dp")
    length = n // 2
    spot = me // 2
    side = lax.rem(me, 2)

    half = buf.shape[1] // PARTS

    def send(piece, h, sem, target):
        at = buf.at[piece, pl.ds(h * half, half)]
        return pltpu.make_async_remote_copy(
            src_ref=at, dst_ref=at, send_sem=sem, recv_sem=recv_sem.at[piece, h],
            device_id={"dp": target}, device_id_type=MESH,
        )

    def arrive(piece, h):
        send(piece, h, side_sem.at[0, h], me).wait_recv()

    def to_right(t, h):
        return send((spot - t) * 2 + side, h, right_sem.at[t, h], me + 2)

    def to_left(t, h):
        return send((spot + t) * 2 + side, h, left_sem.at[t, h], me - 2)

    def across(at, h):
        return send(at * 2 + side, h, side_sem.at[at, h], spot * 2 + 1 - side)

    has_right = spot < length - 1
    has_left = spot > 0
    for t in range(length):
        for h in range(PARTS):
            @pl.when(spot - t >= 0)
            def _():
                if t:
                    arrive((spot - t) * 2 + side, h)

                @pl.when(has_right)
                def _():
                    to_right(t, h).start()

                if t:
                    across(spot - t, h).start()

            @pl.when(spot + t < length)
            def _():
                if t:
                    arrive((spot + t) * 2 + side, h)

                @pl.when(has_left)
                def _():
                    to_left(t, h).start()

                across(spot + t, h).start()

    for h in range(PARTS):
        for at in range(length):
            arrive(at * 2 + 1 - side, h)
            across(at, h).wait_send()
        for t in range(length):
            @pl.when((spot - t >= 0) & has_right)
            def _():
                to_right(t, h).wait_send()

            @pl.when((spot + t < length) & has_left)
            def _():
                to_left(t, h).wait_send()


def line_sems():
    n = lax.axis_size("dp")
    dma = pltpu.SemaphoreType.DMA
    return [dma((n // 2, PARTS)), dma((n // 2, PARTS)), dma((n // 2, PARTS)), dma((n, PARTS))]


def gather_kernel(q_ref, all_ref, own_sem, *sems):
    own = pltpu.make_async_copy(q_ref, all_ref.at[lax.axis_index("dp")], own_sem)
    own.start()
    axis_barrier(("dp",))
    own.wait()
    line_gather(all_ref, *sems)


def gather_queries(queries):
    n = lax.axis_size("dp")
    return pl.pallas_call(
        gather_kernel,
        out_shape=jax.ShapeDtypeStruct((n,) + queries.shape, queries.dtype),
        in_specs=[pl.BlockSpec(memory_space=pltpu.VMEM)],
        out_specs=pl.BlockSpec(memory_space=pltpu.VMEM),
        scratch_shapes=[pltpu.SemaphoreType.DMA] + line_sems(),
        compiler_params=pltpu.CompilerParams(collective_id=0, has_side_effects=True),
    )(queries)


def attend_kernel(
    sizes, codes, counts, totals, q_ref, k_hbm, v_hbm, code_ref, stat_ref,
    acc_ref, kbuf, vbuf, kmore, vmore, ksem, vsem, moresem,
):
    rows, max_pages, span, kv_local, blocks, code_base, unroll = sizes
    q_local, head_dim = q_ref.shape[1:]
    per = 128 // span
    held = per * PRE
    b = pl.program_id(0)
    f32 = jnp.float32

    def issue(block, slot):
        @pl.loop(0, rows)
        def _(r):
            row = block * rows + r

            @pl.loop(0, jnp.minimum(counts[row], held))
            def _(s):
                page = lax.div(codes[row * max_pages + s], code_base)
                pltpu.make_async_copy(k_hbm.at[page], kbuf.at[slot, r * held + s], ksem.at[slot]).start()
                pltpu.make_async_copy(v_hbm.at[page], vbuf.at[slot, r * held + s], vsem.at[slot]).start()

    @pl.when(b == 0)
    def _():
        @pl.loop(0, DEPTH)
        def _(slot):
            @pl.loop(0, rows)
            def _(r):
                vbuf[slot, pl.ds(r * held, held)] = jnp.zeros((held, span, head_dim), vbuf.dtype)

        vmore[...] = jnp.zeros(vmore.shape, vmore.dtype)
        for first in range(min(DEPTH - 1, blocks)):
            issue(first, first)

    @pl.when(b + DEPTH - 1 < blocks)
    def _():
        issue(b + DEPTH - 1, lax.rem(b + DEPTH - 1, DEPTH))

    slot = lax.rem(b, DEPTH)
    total = totals[b]
    for bit in range((rows * held).bit_length()):
        size = 1 << bit
        if size > min(rows * held, k_hbm.shape[0]):
            break

        @pl.when((total >> bit) & 1 == 1)
        def _():
            pltpu.make_async_copy(k_hbm.at[pl.ds(0, size)], kbuf.at[slot, pl.ds(0, size)], ksem.at[slot]).wait()
            pltpu.make_async_copy(v_hbm.at[pl.ds(0, size)], vbuf.at[slot, pl.ds(0, size)], vsem.at[slot]).wait()

    lane = lax.broadcasted_iota(jnp.int32, (per * q_local, 128), 1)
    line = lax.broadcasted_iota(jnp.int32, (per * q_local, 128), 0)
    fits = (lane // span == line // q_local) & (
        lane % kv_local == (line % q_local) // (q_local // kv_local)
    )
    token = jnp.where(fits, (lane % span) // kv_local, code_base)
    stat_lane = lax.broadcasted_iota(jnp.int32, (q_local, 128), 1)
    scale = head_dim ** (-0.5)

    def raw_scores(r, keys):
        return lax.dot_general(
            q_ref[r], keys, (((1,), (1,)), ((), ())), preferred_element_type=f32
        ) * scale

    def chunk(r, first, scores, values):
        row = b * rows + r
        limits = [lax.rem(codes[row * max_pages + first + i], code_base) for i in range(per)]
        limit = jnp.concatenate([jnp.full((q_local, 128), x, jnp.int32) for x in limits], axis=0)
        valid = token < limit
        spread = jnp.where(valid, jnp.concatenate([scores] * per, axis=0), NEG)
        peak = jnp.max(spread, axis=1, keepdims=True)
        weights = jnp.where(valid, jnp.exp(spread - peak), 0.0)
        mass = jnp.sum(weights, axis=1, keepdims=True)
        acc = jnp.dot(weights.astype(jnp.bfloat16), values, preferred_element_type=f32)
        peak = peak.reshape(per, q_local, 1)
        top = jnp.max(peak, axis=0)
        factor = jnp.exp(peak - top[None])
        mass = jnp.sum(mass.reshape(per, q_local, 1) * factor, axis=0)
        acc = jnp.sum(acc.reshape(per, q_local, head_dim) * factor, axis=0)
        return top, mass, acc

    def put_stats(r, stats, top, mass):
        return jnp.where(stat_lane == r, top, stats[0]), jnp.where(stat_lane == r, mass, stats[1])

    def first_chunk(r, stats):
        at = pl.ds(r * held, per)
        top, mass, acc = chunk(
            r, 0, acc_ref[r], vbuf[slot, at].reshape(128, head_dim)
        )
        acc_ref[r] = acc
        return put_stats(r, stats, top, mass)

    def body(i, stats):
        for u in range(unroll):
            stats = first_chunk(i * unroll + u, stats)
        return stats

    @pl.loop(0, rows // unroll)
    def _(i):
        for u in range(unroll):
            r = i * unroll + u
            acc_ref[r] = raw_scores(r, kbuf[slot, pl.ds(r * held, per)].reshape(128, head_dim))

    empty = (jnp.full((q_local, 128), NEG, f32), jnp.zeros((q_local, 128), f32))
    stats = lax.fori_loop(0, rows // unroll, body, empty)
    stat_ref[0], stat_ref[1] = stats

    def merge(r, part):
        top, mass, acc = part
        here = stat_lane == r
        old_top = jnp.max(jnp.where(here, stat_ref[0], NEG), axis=1, keepdims=True)
        old_mass = jnp.sum(jnp.where(here, stat_ref[1], 0.0), axis=1, keepdims=True)
        new_top = jnp.maximum(old_top, top)
        old_f = jnp.exp(old_top - new_top)
        new_f = jnp.exp(top - new_top)
        acc_ref[r] = acc_ref[r] * old_f + acc * new_f
        stat_ref[0] = jnp.where(here, new_top, stat_ref[0])
        stat_ref[1] = jnp.where(here, old_mass * old_f + mass * new_f, stat_ref[1])

    @pl.loop(0, rows)
    def _(r):
        row = b * rows + r
        count = counts[row]

        @pl.when(count > per)
        def _():
            for j in range(1, PRE):
                at = pl.ds(r * held + j * per, per)
                merge(r, chunk(
                    r, j * per,
                    raw_scores(r, kbuf[slot, at].reshape(128, head_dim)),
                    vbuf[slot, at].reshape(128, head_dim),
                ))

            @pl.loop(PRE, jnp.maximum((count + per - 1) // per, PRE))
            def _(j):
                @pl.loop(0, jnp.minimum(count - j * per, per))
                def _(s):
                    page = lax.div(codes[row * max_pages + j * per + s], code_base)
                    first = pltpu.make_async_copy(k_hbm.at[page], kmore.at[s], moresem.at[0])
                    second = pltpu.make_async_copy(v_hbm.at[page], vmore.at[s], moresem.at[1])
                    first.start()
                    second.start()
                    first.wait()
                    second.wait()

                merge(r, chunk(
                    r, j * per, raw_scores(r, kmore[...].reshape(128, head_dim)),
                    vmore[...].reshape(128, head_dim),
                ))

    def encode(i, steps):
        for u in range(unroll):
            r = i * unroll + u
            acc = acc_ref[r]
            step = jnp.max(jnp.abs(acc), axis=1, keepdims=True) * (1.0 / 32767.0)
            floor = jnp.maximum(step, 1e-30)
            inverse = 1.0 / floor
            inverse = jnp.where(step > 1e-30, inverse * (2.0 - floor * inverse), 0.0)
            code_ref[r] = jnp.round(acc * inverse).astype(jnp.int32).astype(jnp.int16)
            steps = jnp.where(stat_lane == r, step, steps)
        return steps

    stat_ref[2] = lax.fori_loop(0, rows // unroll, encode, jnp.zeros((q_local, 128), f32))


def attend(codes, counts, totals, all_queries, keys, values, page_len, kv_local, code_base, max_pages):
    blocks, rows, q_local, head_dim = all_queries.shape
    span = page_len * kv_local
    per = 128 // span
    held = per * PRE
    unroll = 32 if rows % 32 == 0 else 1
    sizes = (rows, max_pages, span, kv_local, blocks, code_base, unroll)
    return pl.pallas_call(
        functools.partial(attend_kernel, sizes),
        out_shape=(
            jax.ShapeDtypeStruct((blocks, rows, q_local, head_dim), jnp.int16),
            jax.ShapeDtypeStruct((blocks, 3, q_local, 128), jnp.float32),
        ),
        grid_spec=pltpu.PrefetchScalarGridSpec(
            num_scalar_prefetch=3,
            grid=(blocks,),
            in_specs=[
                pl.BlockSpec((None, rows, q_local, head_dim), lambda b, *_: (b, 0, 0, 0)),
                pl.BlockSpec(memory_space=pl.ANY),
                pl.BlockSpec(memory_space=pl.ANY),
            ],
            out_specs=(
                pl.BlockSpec((None, rows, q_local, head_dim), lambda b, *_: (b, 0, 0, 0)),
                pl.BlockSpec((None, 3, q_local, 128), lambda b, *_: (b, 0, 0, 0)),
            ),
            scratch_shapes=[
                pltpu.VMEM((rows, q_local, head_dim), jnp.float32),
                pltpu.VMEM((DEPTH, rows * held, span, head_dim), keys.dtype),
                pltpu.VMEM((DEPTH, rows * held, span, head_dim), keys.dtype),
                pltpu.VMEM((per, span, head_dim), keys.dtype),
                pltpu.VMEM((per, span, head_dim), keys.dtype),
                pltpu.SemaphoreType.DMA((DEPTH,)),
                pltpu.SemaphoreType.DMA((DEPTH,)),
                pltpu.SemaphoreType.DMA((2,)),
            ],
        ),
        compiler_params=pltpu.CompilerParams(dimension_semantics=("arbitrary",)),
    )(codes, counts, totals, all_queries, keys, values)


def finish_kernel(
    acc_hbm, stat_hbm, w_hbm, att_out, proj_out,
    got_acc, got_stat, weight, mixed, everyone, part, got_pair, summed, got_part,
    acc_send, acc_recv, stat_send, stat_recv, own_sem, w_sem,
    pair_send, pair_recv, part_send, part_recv,
    right_sem, left_sem, side_sem, line_recv,
):
    n = lax.axis_size("dp")
    me = lax.axis_index("dp")
    m = lax.axis_size("mp")
    mine = lax.axis_index("mp")
    rows, q_local, head_dim = att_out.shape
    out_rows = proj_out.shape[0]
    pieces = pair_send.shape[0]
    width = proj_out.shape[1] // pieces
    load_w = pltpu.make_async_copy(w_hbm, weight, w_sem)
    load_w.start()
    own_acc = pltpu.make_async_copy(acc_hbm.at[me], got_acc.at[0], own_sem.at[0])
    own_stat = pltpu.make_async_copy(stat_hbm.at[me], got_stat.at[0], own_sem.at[1])
    own_acc.start()
    own_stat.start()
    axis_barrier(("dp", "mp"))

    stat_copies, acc_copies = [None], [None]
    for step in range(1, n):
        peer = lax.rem(me + step, n)
        for src, dst, send, recv, copies in (
            (stat_hbm, got_stat, stat_send, stat_recv, stat_copies),
            (acc_hbm, got_acc, acc_send, acc_recv, acc_copies),
        ):
            copies.append(pltpu.make_async_remote_copy(
                src_ref=src.at[peer], dst_ref=dst.at[step],
                send_sem=send.at[step], recv_sem=recv.at[step],
                device_id={"dp": peer}, device_id_type=MESH,
            ))
    for copies in (stat_copies, acc_copies):
        for copy in copies[1:]:
            copy.start()
    own_stat.wait()
    for copy in stat_copies[1:]:
        copy.wait()

    top = got_stat[0, 0]
    for s in range(1, n):
        top = jnp.maximum(top, got_stat[s, 0])
    factors = [jnp.exp(got_stat[s, 0] - top) for s in range(n)]
    mass = factors[0] * got_stat[0, 1]
    for s in range(1, n):
        mass = mass + factors[s] * got_stat[s, 1]
    gains = [factors[s] * got_stat[s, 2] / mass for s in range(n)]
    own_acc.wait()
    for s in range(n):
        if s:
            acc_copies[s].wait()
        for r in range(rows):
            term = gains[s][:, r : r + 1] * got_acc[s, r].astype(jnp.float32)
            mixed[r] = mixed[r] + term if s else term
    att_out[...] = mixed[...].astype(jnp.bfloat16)
    for h in range(q_local):
        everyone[me, :, h * head_dim : (h + 1) * head_dim] = mixed[:, h, :].astype(jnp.bfloat16)

    line_gather(everyone, right_sem, left_sem, side_sem, line_recv)
    load_w.wait()

    pair = lax.rem(mine, 2)
    group = mine // 2
    groups = m // 2

    def pair_copy(piece):
        return pltpu.make_async_remote_copy(
            src_ref=part.at[piece, :, 1 - pair], dst_ref=got_pair.at[piece],
            send_sem=pair_send.at[piece], recv_sem=pair_recv.at[piece],
            device_id={"mp": group * 2 + 1 - pair}, device_id_type=MESH,
        )

    def group_copy(piece, step):
        return pltpu.make_async_remote_copy(
            src_ref=summed.at[piece, step], dst_ref=got_part.at[piece, step],
            send_sem=part_send.at[step, piece], recv_sem=part_recv.at[step, piece],
            device_id={"mp": lax.rem(group + step, groups) * 2 + pair}, device_id_type=MESH,
        )

    flat = everyone[...].reshape(n * rows, q_local * head_dim)
    for piece in range(pieces):
        value = jnp.dot(
            flat, weight[:, piece * width : (piece + 1) * width], preferred_element_type=jnp.float32
        )
        part[piece] = value.reshape(groups, 2, out_rows, width)
        pair_copy(piece).start()
    for piece in range(pieces):
        pair_copy(piece).wait()
        for step in range(groups):
            at = lax.rem(group + step, groups)
            summed[piece, step] = part[piece, at, pair] + got_pair[piece, at]
        for step in range(1, groups):
            group_copy(piece, step).start()
    for piece in range(pieces):
        total = summed[piece, 0]
        for step in range(1, groups):
            group_copy(piece, step).wait()
            total = total + got_part[piece, step]
        proj_out[:, piece * width : (piece + 1) * width] = total.astype(jnp.bfloat16)


def finish(acc, stat, out_weight):
    n, rows, q_local, head_dim = acc.shape
    m = lax.axis_size("mp")
    depth, columns = out_weight.shape
    out_rows = n * rows // m
    pieces = max(columns // 256, 1)
    width = columns // pieces
    dma = pltpu.SemaphoreType.DMA
    return pl.pallas_call(
        finish_kernel,
        out_shape=(
            jax.ShapeDtypeStruct((rows, q_local, head_dim), jnp.bfloat16),
            jax.ShapeDtypeStruct((out_rows, columns), jnp.bfloat16),
        ),
        in_specs=[pl.BlockSpec(memory_space=pl.ANY)] * 3,
        out_specs=(pl.BlockSpec(memory_space=pltpu.VMEM),) * 2,
        scratch_shapes=[
            pltpu.VMEM((n, rows, q_local, head_dim), acc.dtype),
            pltpu.VMEM((n, 3, q_local, 128), jnp.float32),
            pltpu.VMEM((depth, columns), out_weight.dtype),
            pltpu.VMEM((rows, q_local, head_dim), jnp.float32),
            pltpu.VMEM((n, rows, q_local * head_dim), jnp.bfloat16),
            pltpu.VMEM((pieces, m // 2, 2, out_rows, width), jnp.float32),
            pltpu.VMEM((pieces, m // 2, out_rows, width), jnp.float32),
            pltpu.VMEM((pieces, m // 2, out_rows, width), jnp.float32),
            pltpu.VMEM((pieces, m // 2, out_rows, width), jnp.float32),
            dma((n,)), dma((n,)), dma((n,)), dma((n,)), dma((2,)), dma,
            dma((pieces,)), dma((pieces,)), dma((m // 2, pieces)), dma((m // 2, pieces)),
        ] + line_sems(),
        compiler_params=pltpu.CompilerParams(collective_id=1, has_side_effects=True),
    )(acc, stat, out_weight)


def shards(queries, lookup_sheets, content_sheets, page_table, context_len, out_weight):
    req_rows, max_pages = page_table.shape
    pool_local, page_len, kv_local, head_dim = lookup_sheets.shape
    dp_count = lax.axis_size("dp")
    rows_mine = req_rows // dp_count
    code_base = 2 * page_len
    span = page_len * kv_local
    held = (128 // span) * PRE

    local = page_table - lax.axis_index("dp") * pool_local
    slots = jnp.arange(max_pages, dtype=jnp.int32)
    used = jnp.clip(context_len[:, None] - slots[None, :] * page_len, 0, page_len)
    wanted = (local >= 0) & (local < pool_local) & (used > 0)
    before = (slots[:, None] < slots[None, :]).astype(jnp.bfloat16)
    rank = jnp.dot(
        wanted.astype(jnp.bfloat16), before, preferred_element_type=jnp.float32
    ).astype(jnp.int32)
    code = jnp.where(wanted, local * code_base + used, 0)
    rank = jnp.where(wanted, rank, -1)
    codes = jnp.sum(
        jnp.where(rank[:, None, :] == slots[None, :, None], code[:, None, :], 0), axis=2
    )
    counts = jnp.sum(wanted.astype(jnp.int32), axis=1)
    totals = jnp.sum(jnp.minimum(counts, held).reshape(dp_count, rows_mine), axis=1)

    all_queries = gather_queries(queries)
    acc, stat = attend(
        codes.reshape(-1), counts, totals, all_queries,
        lookup_sheets.reshape(pool_local, span, head_dim),
        content_sheets.reshape(pool_local, span, head_dim),
        page_len, kv_local, code_base, max_pages,
    )
    return finish(acc, stat, out_weight)


def solution(mesh):
    placed = (
        P("dp", "mp", None),
        P("dp", None, "mp", None),
        P("dp", None, "mp", None),
        P(),
        P(),
        P("mp", "dp"),
    )
    return jax.shard_map(
        shards,
        mesh=mesh,
        in_specs=placed,
        out_specs=(P("dp", "mp", None), P("mp", "dp")),
        check_vma=False,
    )
```

profile of v0, /device:TPU:4, one launch (start us, length us, event | category | flops | bytes accessed | tf_op | source)
XLA Modules:
  0.0 330.7 jit_solution(15616897878779789173)
XLA Ops:
  0.6 1.1 convert_reduce_fusion
  1.7 0.0 copy-start
  1.7 0.1 min.22
  1.8 0.6 reduce_sum.29.totals
  2.4 1.0 add_select_fusion
  3.5 0.2 fusion
  3.7 0.6 select_reduce_fusion
  4.3 0.2 copy.12
  4.5 0.8 reshape.25.codes
  5.3 69.5 %shard_map.77.q_ref = bf16[32,32,16,128]{3,2,1,0:T(8,128)(2,1)} custom-call(bf16[32,16,128]{2,1,0:T(8,128)(2,1)} %q_ref.1), custom_call_target="tpu_custom_call" | custom-call | tf_op jit(solution)/shard_map/pallas_call | solution.py:116
  74.8 0.0 copy-done
  74.9 82.7 %shard_map.78 = (s16[32,32,16,128]{3,2,1,0:T(8,128)(2,1)}, f32[32,3,16,128]{3,2,1,0:T(8,128)}) custom-call(s32[32768]{0:T(1024)} %reshape.25.codes, s32[1024]{0:T(1024)} %copy-done, s32[32]{0:T(128)} %reduce_sum.29.totals, bf16[32,32,16,128]{3,2,1,0:T(8,128)(2,1)} %shard_map.77.q_ref, bf16[1024,32,128]{2,1,0:T(8,128)(2,1)} %bitcast.3, ...), custom_call_target="tpu_custom_call" | custom-call | tf_op jit(solution)/shard_map/pallas_call | solution.py:299
  157.5 170.1 %shard_map.79 = (bf16[32,16,128]{2,1,0:T(8,128)(2,1)}, bf16[256,256]{1,0:T(8,128)(2,1)}) custom-call(s16[32,32,16,128]{3,2,1,0:T(8,128)(2,1)} %get-tuple-element.4.acc_hbm, f32[32,3,16,128]{3,2,1,0:T(8,128)} %get-tuple-element.5.stat_hbm, bf16[2048,256]{1,0:T(8,128)(2,1)} %w_hbm.1), custom_call_target="tpu_custom_call" | custom-call | tf_op jit(solution)/shard_map/pallas_call | solution.py:444
  327.6 1.6 copy.19
  329.2 1.6 copy.20
  (2 shorter events, 0.0 us)
Async XLA Ops:
  1.7 73.1 %copy-start = (s32[1024]{0:T(1024)}, s32[1024]{0:T(1024)S(1)}, u32[]{:S(2)}) copy-start(s32[1024]{0:T(1024)S(1)} %get-tuple-element.6.counts) | copy-start | bytes 12292
where the time goes:
time: 331 us
  Pallas kernels  322 us (97%)
  local copies, waits for them, and re-layouts  4.24 us (1%)
  other arithmetic  3.33 us (1%)
    pallas_call x1, Pallas kernels, finish(): pl.pallas_call(finish_kernel, out_shape=(jax.ShapeDtypeStruct((rows, q_lo...  170 us
    pallas_call x1, Pallas kernels, attend(): pl.pallas_call(functools.partial(attend_kernel, sizes), out_shape=(jax.Sh...  82.7 us
    pallas_call x1, Pallas kernels, gather_queries(): pl.pallas_call(gather_kernel, out_shape=jax.ShapeDtypeStruct((n,) + queri...  69.5 us

commit v1 on v0

--- a/solution.py
+++ b/solution.py
@@ -11,7 +11,7 @@
 NEG = -1e30
 DEPTH = 4
 PRE = 2
-PARTS = 2
+RING = 4
 
 
 def axis_barrier(axes):
@@ -28,87 +28,100 @@
     pl.semaphore_wait(barrier, total)
 
 
-def line_gather(buf, right_sem, left_sem, side_sem, recv_sem):
-    n = lax.axis_size("dp")
+def place():
     me = lax.axis_index("dp")
-    length = n // 2
-    spot = me // 2
-    side = lax.rem(me, 2)
-
-    half = buf.shape[1] // PARTS
-
-    def send(piece, h, sem, target):
-        at = buf.at[piece, pl.ds(h * half, half)]
+    return lax.rem(me, 2), lax.rem(me // 2, RING), me // (2 * RING)
+
+
+def spot(side, y, z):
+    return (lax.rem(z + RING, RING) * RING + lax.rem(y + RING, RING)) * 2 + side
+
+
+def torus_gather(buf, send_sem, recv_sem):
+    side, y, z = place()
+    me = spot(side, y, z)
+    sent = []
+
+    def piece(q, i, j, of=None):
+        of = side if of is None else of
+        return spot(of, y + i, z + j) if q < 2 else spot(of, y + j, z + i)
+
+    def copy(q, what, target):
+        at = buf.at[what, q]
         return pltpu.make_async_remote_copy(
-            src_ref=at, dst_ref=at, send_sem=sem, recv_sem=recv_sem.at[piece, h],
+            src_ref=at, dst_ref=at, send_sem=send_sem.at[len(sent)], recv_sem=recv_sem.at[what, q],
             device_id={"dp": target}, device_id_type=MESH,
         )
 
-    def arrive(piece, h):
-        send(piece, h, side_sem.at[0, h], me).wait_recv()
-
-    def to_right(t, h):
-        return send((spot - t) * 2 + side, h, right_sem.at[t, h], me + 2)
-
-    def to_left(t, h):
-        return send((spot + t) * 2 + side, h, left_sem.at[t, h], me - 2)
-
-    def across(at, h):
-        return send(at * 2 + side, h, side_sem.at[at, h], spot * 2 + 1 - side)
-
-    has_right = spot < length - 1
-    has_left = spot > 0
-    for t in range(length):
-        for h in range(PARTS):
-            @pl.when(spot - t >= 0)
-            def _():
-                if t:
-                    arrive((spot - t) * 2 + side, h)
-
-                @pl.when(has_right)
-                def _():
-                    to_right(t, h).start()
-
-                if t:
-                    across(spot - t, h).start()
-
-            @pl.when(spot + t < length)
-            def _():
-                if t:
-                    arrive((spot + t) * 2 + side, h)
-
-                @pl.when(has_left)
-                def _():
-                    to_left(t, h).start()
-
-                across(spot + t, h).start()
-
-    for h in range(PARTS):
-        for at in range(length):
-            arrive(at * 2 + 1 - side, h)
-            across(at, h).wait_send()
-        for t in range(length):
-            @pl.when((spot - t >= 0) & has_right)
-            def _():
-                to_right(t, h).wait_send()
-
-            @pl.when((spot + t < length) & has_left)
-            def _():
-                to_left(t, h).wait_send()
-
-
-def line_sems():
+    def send(q, what, target):
+        out = copy(q, what, target)
+        out.start()
+        sent.append(out)
+
+    def take(q, i, j, to=()):
+        what = piece(q, i, j)
+        if (i, j) != (0, 0):
+            copy(q, what, me).wait_recv()
+        for target in to:
+            send(q, what, piece(q, *target))
+        send(q, what, spot(1 - side, y, z))
+
+    both = ((0, 1), (0, -1))
+    for q in range(4):
+        take(q, 0, 0, ((1, 0), (-1, 0)) + both)
+    stages = (
+        (lambda d: (-d, 0), lambda d: ((d, 0),) + both),
+        (lambda d: (d, 0), lambda d: both),
+        (lambda d: (0, -d), lambda d: ((0, d),)),
+        (lambda d: (0, d), lambda d: ()),
+        (lambda d: (2, 0), lambda d: both),
+        (lambda d: (-d, -d), lambda d: ((0, d),)),
+        (lambda d: (d, -d), lambda d: ((0, d),)),
+        (lambda d: (-d, d), lambda d: ()),
+        (lambda d: (d, d), lambda d: ()),
+        (lambda d: (0, 2), lambda d: ()),
+        (lambda d: (2, -d), lambda d: ((0, d),)),
+        (lambda d: (-d, 2), lambda d: ()),
+        (lambda d: (d, 2), lambda d: ()),
+        (lambda d: (2, d), lambda d: ()),
+        (lambda d: (2, 2), lambda d: ()),
+    )
+    for where, to in stages:
+        for q in range(4):
+            d = 1 - 2 * (q % 2)
+            take(q, *where(d), to(d))
+    for i in range(RING):
+        for j in range(RING):
+            for q in range(4):
+                copy(q, spot(1 - side, i, j), me).wait_recv()
+    for out in sent:
+        out.wait_send()
+
+
+def torus_sems():
     n = lax.axis_size("dp")
     dma = pltpu.SemaphoreType.DMA
-    return [dma((n // 2, PARTS)), dma((n // 2, PARTS)), dma((n // 2, PARTS)), dma((n, PARTS))]
+    return [dma((124,)), dma((n, 4))]
+
+
+def near_barrier():
+    side, y, z = place()
+    barrier = pltpu.get_barrier_semaphore()
+    peers = [
+        spot(side, y + 1, z), spot(side, y - 1, z), spot(side, y, z + 1), spot(side, y, z - 1),
+        spot(1 - side, y, z),
+    ]
+    for peer in peers:
+        pl.semaphore_signal(barrier, inc=1, device_id={"dp": peer}, device_id_type=MESH)
+    pl.semaphore_wait(barrier, len(peers))
 
 
 def gather_kernel(q_ref, all_ref, own_sem, *sems):
     own = pltpu.make_async_copy(q_ref, all_ref.at[lax.axis_index("dp")], own_sem)
     own.start()
-    axis_barrier(("dp",))
+    near_barrier()
     own.wait()
-    line_gather(all_ref, *sems)
+    torus_gather(all_ref, *sems)
 
 
 def gather_queries(queries):
@@ -118,7 +131,7 @@
         out_shape=jax.ShapeDtypeStruct((n,) + queries.shape, queries.dtype),
         in_specs=[pl.BlockSpec(memory_space=pltpu.VMEM)],
         out_specs=pl.BlockSpec(memory_space=pltpu.VMEM),
-        scratch_shapes=[pltpu.SemaphoreType.DMA] + line_sems(),
+        scratch_shapes=[pltpu.SemaphoreType.DMA] + torus_sems(),
         compiler_params=pltpu.CompilerParams(collective_id=0, has_side_effects=True),
     )(queries)
 
@@ -334,7 +347,7 @@
     got_acc, got_stat, weight, mixed, everyone, part, got_pair, summed, got_part,
     acc_send, acc_recv, stat_send, stat_recv, own_sem, w_sem,
     pair_send, pair_recv, part_send, part_recv,
-    right_sem, left_sem, side_sem, line_recv,
+    torus_send, torus_recv,
 ):
     n = lax.axis_size("dp")
     me = lax.axis_index("dp")
@@ -388,9 +401,10 @@
             mixed[r] = mixed[r] + term if s else term
     att_out[...] = mixed[...].astype(jnp.bfloat16)
     for h in range(q_local):
-        everyone[me, :, h * head_dim : (h + 1) * head_dim] = mixed[:, h, :].astype(jnp.bfloat16)
-
-    line_gather(everyone, right_sem, left_sem, side_sem, line_recv)
+        at = (h % 4) * head_dim
+        everyone[me, h // 4, :, at : at + head_dim] = mixed[:, h, :].astype(jnp.bfloat16)
+
+    torus_gather(everyone, torus_send, torus_recv)
     load_w.wait()
 
     pair = lax.rem(mine, 2)
@@ -411,11 +425,15 @@
             device_id={"mp": lax.rem(group + step, groups) * 2 + pair}, device_id_type=MESH,
         )
 
-    flat = everyone[...].reshape(n * rows, q_local * head_dim)
+    band = q_local * head_dim // 4
     for piece in range(pieces):
-        value = jnp.dot(
-            flat, weight[:, piece * width : (piece + 1) * width], preferred_element_type=jnp.float32
-        )
+        value = 0.0
+        for q in range(4):
+            value += jnp.dot(
+                everyone[:, q].reshape(n * rows, band),
+                weight[q * band : (q + 1) * band, piece * width : (piece + 1) * width],
+                preferred_element_type=jnp.float32,
+            )
         part[piece] = value.reshape(groups, 2, out_rows, width)
         pair_copy(piece).start()
     for piece in range(pieces):
@@ -454,14 +472,14 @@
             pltpu.VMEM((n, 3, q_local, 128), jnp.float32),
             pltpu.VMEM((depth, columns), out_weight.dtype),
             pltpu.VMEM((rows, q_local, head_dim), jnp.float32),
-            pltpu.VMEM((n, rows, q_local * head_dim), jnp.bfloat16),
+            pltpu.VMEM((n, 4, rows, q_local * head_dim // 4), jnp.bfloat16),
             pltpu.VMEM((pieces, m // 2, 2, out_rows, width), jnp.float32),
             pltpu.VMEM((pieces, m // 2, out_rows, width), jnp.float32),
             pltpu.VMEM((pieces, m // 2, out_rows, width), jnp.float32),
             pltpu.VMEM((pieces, m // 2, out_rows, width), jnp.float32),
             dma((n,)), dma((n,)), dma((n,)), dma((n,)), dma((2,)), dma,
             dma((pieces,)), dma((pieces,)), dma((m // 2, pieces)), dma((m // 2, pieces)),
-        ] + line_sems(),
+        ] + torus_sems(),
         compiler_params=pltpu.CompilerParams(collective_id=1, has_side_effects=True),
     )(acc, stat, out_weight)
 
@@ -491,7 +509,8 @@
     counts = jnp.sum(wanted.astype(jnp.int32), axis=1)
     totals = jnp.sum(jnp.minimum(counts, held).reshape(dp_count, rows_mine), axis=1)
 
-    all_queries = gather_queries(queries)
+    all_queries = gather_queries(queries.reshape(4, rows_mine // 4, *queries.shape[1:]))
+    all_queries = all_queries.reshape(dp_count, *queries.shape)
     acc, stat = attend(
         codes.reshape(-1), counts, totals, all_queries,
         lookup_sheets.reshape(pool_local, span, head_dim),

time: 331 us -> 248 us (0.75)
  Pallas kernels: 322 us -> 238 us
    pallas_call x1, Pallas kernels: 69.5 us -> 26.4 us  [gather_queries(): pl.pallas_call(gather_kernel, out_shape=jax.ShapeDtypeStruct((n,) + queri...]
    pallas_call x1, Pallas kernels: 170 us -> 129 us  [finish(): pl.pallas_call(finish_kernel, out_shape=(jax.ShapeDtypeStruct((rows, q_lo...]
where the time goes in v1:
time: 248 us; the launch traced here: 247 us
  Pallas kernels  238 us (96%)
  local copies, waits for them, and re-layouts  4.24 us (2%)
  other arithmetic  3.33 us (1%)
    pallas_call x1, Pallas kernels, finish(): pl.pallas_call(finish_kernel, out_shape=(jax.ShapeDtypeStruct((rows, q_lo...  129 us
    pallas_call x1, Pallas kernels, attend(): pl.pallas_call(functools.partial(attend_kernel, sizes), out_shape=(jax.Sh...  82.8 us
    pallas_call x1, Pallas kernels, gather_queries(): pl.pallas_call(gather_kernel, out_shape=jax.ShapeDtypeStruct((n,) + queri...  26.4 us

profile of v1, /device:TPU:4, one launch (start us, length us, event | category | flops | bytes accessed | tf_op | source)
XLA Modules:
  0.0 246.6 jit_solution(4063123185318206586)
XLA Ops:
  0.6 1.1 convert_reduce_fusion
  1.7 0.0 copy-start
  1.7 0.1 min.22
  1.8 0.6 reduce_sum.29.totals
  2.4 1.0 add_select_fusion
  3.5 0.2 fusion
  3.7 0.6 select_reduce_fusion
  4.3 0.2 copy.12
  4.5 0.8 reshape.31.codes
  5.3 26.4 %shard_map.77 = bf16[32,4,8,16,128]{4,3,2,1,0:T(8,128)(2,1)} custom-call(bf16[4,8,16,128]{3,2,1,0:T(8,128)(2,1)} %bitcast.8), custom_call_target="tpu_custom_call" | custom-call | tf_op jit(solution)/shard_map/pallas_call | solution.py:129
  31.7 0.0 copy-done
  31.7 82.8 %shard_map.78 = (s16[32,32,16,128]{3,2,1,0:T(8,128)(2,1)}, f32[32,3,16,128]{3,2,1,0:T(8,128)}) custom-call(s32[32768]{0:T(1024)} %reshape.31.codes, s32[1024]{0:T(1024)} %copy-done, s32[32]{0:T(128)} %reduce_sum.29.totals, bf16[32,32,16,128]{3,2,1,0:T(8,128)(2,1)} %bitcast.5, bf16[1024,32,128]{2,1,0:T(8,128)(2,1)} %bitcast.6, bf16[1024,32,128]{2,1,0:T(8,128)(2,1)} %bitcast.7), custom_call_target="tpu_custom_call" | custom-call | tf_op jit(solution)/shard_map/pallas_call | solution.py:312
  114.5 128.9 %shard_map.79 = (bf16[32,16,128]{2,1,0:T(8,128)(2,1)}, bf16[256,256]{1,0:T(8,128)(2,1)}) custom-call(s16[32,32,16,128]{3,2,1,0:T(8,128)(2,1)} %get-tuple-element.4.acc_hbm, f32[32,3,16,128]{3,2,1,0:T(8,128)} %get-tuple-element.5.stat_hbm, bf16[2048,256]{1,0:T(8,128)(2,1)} %w_hbm.1), custom_call_target="tpu_custom_call" | custom-call | tf_op jit(solution)/shard_map/pallas_call | solution.py:462
  243.5 1.6 copy.19
  245.0 1.6 copy.20
  (2 shorter events, 0.0 us)
Async XLA Ops:
  1.7 30.0 %copy-start = (s32[1024]{0:T(1024)}, s32[1024]{0:T(1024)S(1)}, u32[]{:S(2)}) copy-start(s32[1024]{0:T(1024)S(1)} %get-tuple-element.6.counts) | copy-start | bytes 12292

commit v2 on v1

v2 whole, which is shorter than its diff:
```python
import functools

import jax
import jax.numpy as jnp
from jax import lax
from jax.experimental import pallas as pl
from jax.experimental.pallas import tpu as pltpu
from jax.sharding import PartitionSpec as P

MESH = pl.DeviceIdType.MESH
NEG = -1e30
RING = 4
LISTED = 2048
GROUP = 4
UNROLL = 4


def place():
    me = lax.axis_index("dp")
    return lax.rem(me, 2), lax.rem(me // 2, RING), me // (2 * RING)


def around(i):
    return lax.rem(i + RING, RING)


def spot(side, y, z):
    return (around(z) * RING + around(y)) * 2 + side


def remote(src, dst, send, recv, target):
    return pltpu.make_async_remote_copy(
        src_ref=src, dst_ref=dst, send_sem=send, recv_sem=recv,
        device_id=target, device_id_type=MESH,
    )


def greet(peers):
    barrier = pltpu.get_barrier_semaphore()
    for peer in peers:
        pl.semaphore_signal(barrier, inc=1, device_id=peer, device_id_type=MESH)
    pl.semaphore_wait(barrier, len(peers))


def near():
    side, y, z = place()
    return [
        {"dp": spot(side, y + 1, z)}, {"dp": spot(side, y - 1, z)},
        {"dp": spot(side, y, z + 1)}, {"dp": spot(side, y, z - 1)},
        {"dp": spot(1 - side, y, z)},
    ]


def torus_gather(view, send_sem, recv_sem, filler=None):
    side, y, z = place()
    sent = []

    def piece(q, i, j):
        return (side, y + i, z + j) if q < 2 else (side, y + j, z + i)

    def copy(q, what, target):
        at = view(q, *what)
        return remote(at, at, send_sem.at[len(sent)], recv_sem.at[spot(*what), q], {"dp": target})

    def send(q, what, target):
        out = copy(q, what, target)
        out.start()
        sent.append(out)

    def take(q, i, j, to=()):
        what = piece(q, i, j)
        if (i, j) != (0, 0):
            copy(q, what, spot(side, y, z)).wait_recv()
        for target in to:
            send(q, what, spot(*piece(q, *target)))
        send(q, what, spot(1 - side, y, z))

    both = ((0, 1), (0, -1))
    for q in range(4):
        take(q, 0, 0, ((1, 0), (-1, 0)) + both)
    if filler is not None:
        filler()
    stages = (
        (lambda d: (-d, 0), lambda d: ((d, 0),) + both),
        (lambda d: (d, 0), lambda d: both),
        (lambda d: (0, -d), lambda d: ((0, d),)),
        (lambda d: (0, d), lambda d: ()),
        (lambda d: (2, 0), lambda d: both),
        (lambda d: (-d, -d), lambda d: ((0, d),)),
        (lambda d: (d, -d), lambda d: ((0, d),)),
        (lambda d: (-d, d), lambda d: ()),
        (lambda d: (d, d), lambda d: ()),
        (lambda d: (0, 2), lambda d: ()),
        (lambda d: (2, -d), lambda d: ((0, d),)),
        (lambda d: (-d, 2), lambda d: ()),
        (lambda d: (d, 2), lambda d: ()),
        (lambda d: (2, d), lambda d: ()),
        (lambda d: (2, 2), lambda d: ()),
    )
    for where, to in stages:
        for q in range(4):
            d = 1 - 2 * (q % 2)
            take(q, *where(d), to(d))
    for i in range(RING):
        for j in range(RING):
            for q in range(4):
                copy(q, (1 - side, i, j), spot(side, y, z)).wait_recv()
    for out in sent:
        out.wait_send()


def torus_sems():
    n = lax.axis_size("dp")
    dma = pltpu.SemaphoreType.DMA
    return [dma((124,)), dma((n, 4))]


def plan(sizes, table_ref, len_ref, list_ref, pos_ref, code_ref):
    pool_local, page_len = sizes
    slots, rows = table_ref.shape
    f32, bf16, i32 = jnp.float32, jnp.bfloat16, jnp.int32

    def iota(shape, dim):
        return lax.broadcasted_iota(i32, shape, dim)

    def ones(mask):
        return jnp.where(mask, 1.0, 0.0)

    local = table_ref[...] - lax.axis_index("dp") * pool_local
    used = jnp.clip(len_ref[...] - iota((slots, rows), 0) * page_len, 0, page_len)
    wanted = (local >= 0) & (local < pool_local) & (used > 0)
    flags = ones(wanted)
    lower = ones(iota((slots, slots), 1) < iota((slots, slots), 0)).astype(bf16)
    rank = jnp.dot(lower, flags.astype(bf16), preferred_element_type=f32)
    count = jnp.sum(flags, axis=0, keepdims=True)
    some = jnp.minimum(count, 1.0)
    extra = jnp.maximum(count - 1.0, 0.0)
    both = jnp.where(iota((8, rows), 0) == 0, some, extra).astype(bf16)
    upper = ones(iota((rows, rows), 0) < iota((rows, rows), 1)).astype(bf16)
    ahead = jnp.dot(both, upper, preferred_element_type=f32)
    pos = jnp.where(rank == 0.0, ahead[0:1], (LISTED - 1) - ahead[1:2] - (rank - 1.0))
    pos_ref[...] = jnp.where(wanted, pos, -1.0).astype(i32)

    t = iota((1, rows), 1)
    q, turn, y, z = (t >> 3) & 3, (t >> 5) & 1, (t >> 6) & 3, (t >> 8) & 3
    f = jnp.where(q < 2, y, z)
    g = jnp.where(q < 2, z, y)
    row = (q << 8) | (f << 6) | (turn << 5) | (g << 3) | (t & 7)
    code_ref[...] = jnp.where(wanted, (row << 15) | (local << 5) | used, 0)

    high = iota((LISTED // 128, rows), 0)
    low = iota((128, rows), 0)

    def collect(s, total):
        p = pos_ref[pl.ds(s, 1)]
        c = code_ref[pl.ds(s, 1)]
        hit = high == (p >> 7)
        bytes_of = [jnp.where(hit, ((c >> (8 * k)) & 255).astype(f32), 0.0) for k in range(4)]
        left = jnp.concatenate(bytes_of, axis=0).astype(bf16)
        right = ones(low == (p & 127)).astype(bf16)
        return total + lax.dot_general(
            left, right, (((1,), (1,)), ((), ())), preferred_element_type=f32
        )

    height = LISTED // 128
    total = lax.fori_loop(0, slots, collect, jnp.zeros((4 * height, 128), f32)).astype(i32)
    out = total[:height]
    for k in range(1, 4):
        out = out + total[k * height : (k + 1) * height] * (1 << (8 * k))
    list_ref[0:height] = jnp.where(out == 0, rows << 15, out)
    sums = jnp.where(
        iota((8, 128), 0) == 0, jnp.sum(some, axis=1, keepdims=True),
        jnp.sum(extra, axis=1, keepdims=True),
    )
    list_ref[height : height + 8] = sums.astype(i32)


def gather_kernel(
    sizes, q_ref, table_ref, len_ref, all_ref, list_ref, pos_ref, code_ref, own_sem, send, recv
):
    side, y, z = place()

    def view(q, of, at_y, at_z):
        f, g = (at_y, at_z) if q < 2 else (at_z, at_y)
        return all_ref.at[q, around(f), of, around(g)]

    own = [
        pltpu.make_async_copy(q_ref.at[q], view(q, side, y, z), own_sem.at[q]) for q in range(4)
    ]
    for copy in own:
        copy.start()
    greet(near())
    for copy in own:
        copy.wait()
    torus_gather(
        view, send, recv,
        lambda: plan(sizes, table_ref, len_ref, list_ref, pos_ref, code_ref),
    )


def gather_queries(queries, table, lengths, sizes):
    rows, q_local, head_dim = queries.shape
    dma = pltpu.SemaphoreType.DMA
    vmem = pl.BlockSpec(memory_space=pltpu.VMEM)
    return pl.pallas_call(
        functools.partial(gather_kernel, sizes),
        out_shape=(
            jax.ShapeDtypeStruct((4, RING, 2, RING, rows // 4, q_local, head_dim), queries.dtype),
            jax.ShapeDtypeStruct((LISTED // 128 + 8, 128), jnp.int32),
        ),
        in_specs=[vmem] * 3,
        out_specs=(vmem, vmem),
        scratch_shapes=[
            pltpu.VMEM(table.shape, jnp.int32), pltpu.VMEM(table.shape, jnp.int32), dma((4,)),
        ] + torus_sems(),
        compiler_params=pltpu.CompilerParams(collective_id=0, has_side_effects=True),
    )(queries.reshape(4, rows // 4, q_local, head_dim), table, lengths)


def attend_kernel(sizes, listed, q_ref, k_hbm, v_hbm, acc_ref, stat_ref, kbuf, vbuf, sem):
    kv_local, blocks = sizes
    rows, q_local, head_dim = q_ref.shape
    pages, span, _ = k_hbm.shape
    f32, i32 = jnp.float32, jnp.int32
    tall = GROUP * q_local
    wide = GROUP * span
    loads = []
    for src, dst, i in ((k_hbm, kbuf, 0), (v_hbm, vbuf, 1)):
        loads.append(pltpu.make_async_copy(src, dst, sem.at[i]))
    for load in loads:
        load.start()

    @pl.loop(0, blocks)
    def _(b):
        acc_ref[b] = jnp.zeros(acc_ref.shape[1:], f32)
        stat_ref[b, 0] = jnp.full((q_local, 128), NEG, f32)
        stat_ref[b, 1] = jnp.zeros((q_local, 128), f32)

    for load in loads:
        load.wait()

    lane = lax.broadcasted_iota(i32, (tall, wide), 1)
    line = lax.broadcasted_iota(i32, (tall, wide), 0)
    fits = (lane // span == line // q_local) & (
        lane % kv_local == (line % q_local) // (q_local // kv_local)
    )
    token = jnp.where(fits, (lane % span) // kv_local, 64)
    stat_lane = lax.broadcasted_iota(i32, (q_local, 128), 1)
    scale = head_dim ** (-0.5)
    in_block = rows // (blocks - 1)

    def chunk(first):
        codes = [listed[first + i] for i in range(GROUP)]
        used = [code & 31 for code in codes]
        page = [(code >> 5) & (pages - 1) for code in codes]
        row = [code >> 15 for code in codes]
        asked = jnp.concatenate([q_ref[r & (rows - 1)] for r in row], axis=0)
        keys = jnp.concatenate([kbuf[p] for p in page], axis=0)
        values = jnp.concatenate([vbuf[p] for p in page], axis=0)
        scores = lax.dot_general(
            asked, keys, (((1,), (1,)), ((), ())), preferred_element_type=f32
        ) * scale
        limit = jnp.concatenate([jnp.full((q_local, wide), u, i32) for u in used], axis=0)
        valid = token < limit
        scores = jnp.where(valid, scores, NEG)
        peak = jnp.max(scores, axis=1, keepdims=True)
        weights = jnp.where(valid, jnp.exp(scores - peak), 0.0)
        mass = jnp.sum(weights, axis=1, keepdims=True)
        acc = jnp.dot(weights.astype(jnp.bfloat16), values, preferred_element_type=f32)
        return [
            (row[i], peak[i * q_local : (i + 1) * q_local], mass[i * q_local : (i + 1) * q_local],
             acc[i * q_local : (i + 1) * q_local])
            for i in range(GROUP)
        ]

    first_count = listed[LISTED]
    more_count = listed[LISTED + 128]
    step = GROUP * UNROLL

    @pl.loop(0, (first_count + step - 1) // step)
    def _(i):
        parts = []
        for u in range(UNROLL):
            parts += chunk(i * step + u * GROUP)
        for row, peak, mass, acc in parts:
            block, at = row // in_block, lax.rem(row, in_block)
            here = stat_lane == at
            acc_ref[block, at] = acc
            stat_ref[block, 0] = jnp.where(here, peak, stat_ref[block, 0])
            stat_ref[block, 1] = jnp.where(here, mass, stat_ref[block, 1])

    @pl.loop(0, (more_count + GROUP - 1) // GROUP)
    def _(i):
        for row, peak, mass, acc in chunk(LISTED - GROUP - i * GROUP):
            block, at = row // in_block, lax.rem(row, in_block)
            here = stat_lane == at
            old_peak = jnp.max(jnp.where(here, stat_ref[block, 0], NEG), axis=1, keepdims=True)
            old_mass = jnp.sum(jnp.where(here, stat_ref[block, 1], 0.0), axis=1, keepdims=True)
            top = jnp.maximum(old_peak, peak)
            old_f = jnp.exp(old_peak - top)
            new_f = jnp.exp(peak - top)
            acc_ref[block, at] = acc_ref[block, at] * old_f + acc * new_f
            stat_ref[block, 0] = jnp.where(here, top, stat_ref[block, 0])
            stat_ref[block, 1] = jnp.where(here, old_mass * old_f + mass * new_f, stat_ref[block, 1])


def attend(listed, queries, keys, values, kv_local):
    rows, q_local, head_dim = queries.shape
    blocks = rows // 32 + 1
    vmem = pl.BlockSpec(memory_space=pltpu.VMEM)
    hbm = pl.BlockSpec(memory_space=pl.ANY)
    return pl.pallas_call(
        functools.partial(attend_kernel, (kv_local, blocks)),
        out_shape=(
            jax.ShapeDtypeStruct((blocks, 32, q_local, head_dim), jnp.float32),
            jax.ShapeDtypeStruct((blocks, 2, q_local, 128), jnp.float32),
        ),
        in_specs=[pl.BlockSpec(memory_space=pltpu.SMEM), vmem, hbm, hbm],
        out_specs=(vmem, vmem),
        scratch_shapes=[
            pltpu.VMEM(keys.shape, keys.dtype),
            pltpu.VMEM(values.shape, values.dtype),
            pltpu.SemaphoreType.DMA((2,)),
        ],
    )(listed, queries, keys, values)


def finish_kernel(
    acc_hbm, stat_hbm, w_hbm, att_out, proj_out,
    own_acc, own_stat, got_acc, got_stat, out_code, out_stat, in_code, in_stat,
    last_code, last_stat, weight, mixed, everyone, part, got_pair, summed, got_part,
    own_sem, cross_send, cross_recv, hop_send, hop_recv, last_send, last_recv, w_sem,
    pair_send, pair_recv, part_send, part_recv,
    torus_send, torus_recv,
):
    n = lax.axis_size("dp")
    me = lax.axis_index("dp")
    m = lax.axis_size("mp")
    mine = lax.axis_index("mp")
    side, y, z = place()
    rows, q_local, head_dim = att_out.shape
    out_rows = proj_out.shape[0]
    pieces = pair_send.shape[0]
    width = proj_out.shape[1] // pieces
    f32 = jnp.float32
    load_w = pltpu.make_async_copy(w_hbm, weight, w_sem)
    load_w.start()

    def axes(q):
        return jnp.where(q < 2, y, z), jnp.where(q < 2, z, y), 1 - 2 * lax.rem(q, 2)

    def first_axis(q, i):
        return {"dp": jnp.where(q < 2, spot(side, y + i, z), spot(side, y, z + i))}

    def second_axis(q, i):
        return {"dp": jnp.where(q < 2, spot(side, y, z + i), spot(side, y + i, z))}

    def block_of(kind, q, of):
        f, _, d = axes(q)
        f = around(f + jnp.where(kind == 0, 2, jnp.where(kind == 1, -d, jnp.where(kind == 2, d, 0))))
        return (q * RING + f) * 2 + of

    def own_copies(kind, q):
        at = block_of(kind, q, side)
        return (
            pltpu.make_async_copy(acc_hbm.at[at], own_acc.at[kind, q], own_sem.at[0, kind, q]),
            pltpu.make_async_copy(stat_hbm.at[at], own_stat.at[kind, q], own_sem.at[1, kind, q]),
        )

    def cross_copies(kind, q):
        at = block_of(kind, q, 1 - side)
        peer = {"dp": spot(1 - side, y, z)}
        return (
            remote(acc_hbm.at[at], got_acc.at[kind, q], cross_send.at[0, kind, q],
                   cross_recv.at[0, kind, q], peer),
            remote(stat_hbm.at[at], got_stat.at[kind, q], cross_send.at[1, kind, q],
                   cross_recv.at[1, kind, q], peer),
        )

    def hop_copies(kind, q):
        _, _, d = axes(q)
        peer = first_axis(q, jnp.where(kind == 1, -d, d))
        return (
            remote(out_code.at[kind, q], in_code.at[kind, q], hop_send.at[0, kind, q],
                   hop_recv.at[0, kind, q], peer),
            remote(out_stat.at[kind, q], in_stat.at[kind, q], hop_send.at[1, kind, q],
                   hop_recv.at[1, kind, q], peer),
        )

    eighth = rows // 4

    def last_copies(o, q):
        _, g, _ = axes(q)
        peer = second_axis(q, o)
        return (
            remote(out_code.at[3, q, pl.ds(around(g + o) * eighth, eighth)], last_code.at[o - 1, q],
                   last_send.at[0, o - 1, q], last_recv.at[0, o - 1, q], peer),
            remote(out_stat.at[3, q], last_stat.at[o - 1, q],
                   last_send.at[1, o - 1, q], last_recv.at[1, o - 1, q], peer),
        )

    @pl.loop(0, 16)
    def _(i):
        for copy in own_copies(i // 4, lax.rem(i, 4)):
            copy.start()

    peers = near() + [{"dp": spot(side, y + 2, z)}, {"dp": spot(side, y, z + 2)}]
    peers += [{"mp": lax.rem(mine + i, m)} for i in range(1, m)]
    greet(peers)

    @pl.loop(0, 16)
    def _(i):
        for copy in cross_copies(i // 4, lax.rem(i, 4)):
            copy.start()

    stat_lane = lax.broadcasted_iota(jnp.int32, (q_local, 128), 1)

    def aside(tile, by):
        return pltpu.roll(tile, by % 128, 1)

    def combine(tops, masses, steps):
        top = tops[0]
        for other in tops[1:]:
            top = jnp.maximum(top, other)
        mass = 0.0
        gains = []
        for each, its_mass, step in zip(tops, masses, steps):
            factor = jnp.exp(each - top)
            mass = mass + factor * its_mass
            gains.append(factor if step is None else factor * step)
        return top, mass, gains

    def gathered(kind, q, arrived):
        for copy in own_copies(kind, q):
            copy.wait()
        for copy in cross_copies(kind, q):
            copy.wait_recv()
        tops = [own_stat[kind, q, 0], got_stat[kind, q, 0]]
        masses = [own_stat[kind, q, 1], got_stat[kind, q, 1]]
        steps = [None, None]
        for other in arrived:
            for copy in hop_copies(other, q):
                copy.wait_recv()
            tile = in_stat[other, q]
            tops.append(tile)
            masses.append(aside(tile, -32))
            steps.append(aside(tile, -64))
        top, mass, gains = combine(tops, masses, steps)
        step_tile = jnp.zeros((q_local, 128), f32)
        for r in range(rows):
            value = own_acc[kind, q, r] * gains[0][:, r : r + 1]
            value = value + got_acc[kind, q, r] * gains[1][:, r : r + 1]
            for k, other in enumerate(arrived):
                value = value + in_code[other, q, r].astype(f32) * gains[2 + k][:, r : r + 1]
            step = jnp.max(jnp.abs(value), axis=1, keepdims=True) * (1.0 / 32767.0)
            floor = jnp.maximum(step, 1e-30)
            inverse = 1.0 / floor
            inverse = jnp.where(step > 1e-30, inverse * (2.0 - floor * inverse), 0.0)
            out_code[kind, q, r] = jnp.round(value * inverse).astype(jnp.int32).astype(jnp.int16)
            step_tile = jnp.where(stat_lane == r, step, step_tile)
        out_stat[kind, q] = jnp.where(
            stat_lane < 32, top,
            jnp.where(stat_lane < 64, aside(mass, 32), aside(step_tile, 64)),
        )

    @pl.loop(0, 8)
    def _(i):
        kind, q = i // 4, lax.rem(i, 4)
        gathered(kind, q, ())
        for copy in hop_copies(kind, q):
            copy.start()

    @pl.loop(0, 4)
    def _(q):
        gathered(2, q, (0,))
        for copy in hop_copies(2, q):
            copy.start()

    @pl.loop(0, 4)
    def _(q):
        gathered(3, q, (1, 2))
        for o in (1, 3, 2):
            for copy in last_copies(o, q):
                copy.start()

    @pl.loop(0, 4)
    def _(q):
        _, g, _ = axes(q)
        shift = lax.rem(128 - g * eighth, 128)
        tiles = [out_stat[3, q]]
        for o in range(1, 4):
            for copy in last_copies(o, q):
                copy.wait_recv()
            tiles.append(last_stat[o - 1, q])
        tiles = [pltpu.roll(tile, shift, 1) for tile in tiles]
        _, mass, gains = combine(
            tiles, [aside(tile, -32) for tile in tiles], [aside(tile, -64) for tile in tiles]
        )
        gains = [gain / mass for gain in gains]
        for r in range(eighth):
            value = out_code[3, q, g * eighth + r].astype(f32) * gains[0][:, r : r + 1]
            for o in range(1, 4):
                value = value + last_code[o - 1, q, r].astype(f32) * gains[o][:, r : r + 1]
            mixed[q * eighth + r] = value

    att_out[...] = mixed[...].astype(jnp.bfloat16)
    for h in range(q_local):
        at = (h % 4) * head_dim
        everyone[me, h // 4, :, at : at + head_dim] = mixed[:, h, :].astype(jnp.bfloat16)

    torus_gather(lambda q, of, at_y, at_z: everyone.at[spot(of, at_y, at_z), q], torus_send, torus_recv)
    load_w.wait()

    pair = lax.rem(mine, 2)
    group = mine // 2
    groups = m // 2

    def pair_copy(piece):
        return remote(
            part.at[piece, :, 1 - pair], got_pair.at[piece], pair_send.at[piece],
            pair_recv.at[piece], {"mp": group * 2 + 1 - pair},
        )

    def group_copy(piece, step):
        return remote(
            summed.at[piece, step], got_part.at[piece, step], part_send.at[step, piece],
            part_recv.at[step, piece], {"mp": lax.rem(group + step, groups) * 2 + pair},
        )

    band = q_local * head_dim // 4
    for piece in range(pieces):
        value = 0.0
        for q in range(4):
            value += jnp.dot(
                everyone[:, q].reshape(n * rows, band),
                weight[q * band : (q + 1) * band, piece * width : (piece + 1) * width],
                preferred_element_type=f32,
            )
        part[piece] = value.reshape(groups, 2, out_rows, width)
        pair_copy(piece).start()
    for piece in range(pieces):
        pair_copy(piece).wait()
        for step in range(groups):
            at = lax.rem(group + step, groups)
            summed[piece, step] = part[piece, at, pair] + got_pair[piece, at]
        for step in range(1, groups):
            group_copy(piece, step).start()
    for piece in range(pieces):
        total = summed[piece, 0]
        for step in range(1, groups):
            group_copy(piece, step).wait()
            total = total + got_part[piece, step]
        proj_out[:, piece * width : (piece + 1) * width] = total.astype(jnp.bfloat16)

    @pl.loop(0, 16)
    def _(i):
        for copy in cross_copies(i // 4, lax.rem(i, 4)):
            copy.wait_send()

    @pl.loop(0, 12)
    def _(i):
        kind, q = i // 4, lax.rem(i, 4)
        for copy in hop_copies(kind, q) + last_copies(kind + 1, q):
            copy.wait_send()


def finish(acc, stat, out_weight):
    _, rows, q_local, head_dim = acc.shape
    n = lax.axis_size("dp")
    m = lax.axis_size("mp")
    depth, columns = out_weight.shape
    out_rows = n * rows // m
    pieces = max(columns // 256, 1)
    width = columns // pieces
    dma = pltpu.SemaphoreType.DMA
    f32, i16 = jnp.float32, jnp.int16
    return pl.pallas_call(
        finish_kernel,
        out_shape=(
            jax.ShapeDtypeStruct((rows, q_local, head_dim), jnp.bfloat16),
            jax.ShapeDtypeStruct((out_rows, columns), jnp.bfloat16),
        ),
        in_specs=[pl.BlockSpec(memory_space=pl.ANY)] * 3,
        out_specs=(pl.BlockSpec(memory_space=pltpu.VMEM),) * 2,
        scratch_shapes=[
            pltpu.VMEM((4, 4, rows, q_local, head_dim), f32),
            pltpu.VMEM((4, 4, 2, q_local, 128), f32),
            pltpu.VMEM((4, 4, rows, q_local, head_dim), f32),
            pltpu.VMEM((4, 4, 2, q_local, 128), f32),
            pltpu.VMEM((4, 4, rows, q_local, head_dim), i16),
            pltpu.VMEM((4, 4, q_local, 128), f32),
            pltpu.VMEM((3, 4, rows, q_local, head_dim), i16),
            pltpu.VMEM((3, 4, q_local, 128), f32),
            pltpu.VMEM((3, 4, rows // 4, q_local, head_dim), i16),
            pltpu.VMEM((3, 4, q_local, 128), f32),
            pltpu.VMEM((depth, columns), out_weight.dtype),
            pltpu.VMEM((rows, q_local, head_dim), f32),
            pltpu.VMEM((n, 4, rows, q_local * head_dim // 4), jnp.bfloat16),
            pltpu.VMEM((pieces, m // 2, 2, out_rows, width), f32),
            pltpu.VMEM((pieces, m // 2, out_rows, width), f32),
            pltpu.VMEM((pieces, m // 2, out_rows, width), f32),
            pltpu.VMEM((pieces, m // 2, out_rows, width), f32),
            dma((2, 4, 4)), dma((2, 4, 4)), dma((2, 4, 4)),
            dma((2, 3, 4)), dma((2, 3, 4)), dma((2, 3, 4)), dma((2, 3, 4)), dma,
            dma((pieces,)), dma((pieces,)), dma((m // 2, pieces)), dma((m // 2, pieces)),
        ] + torus_sems(),
        compiler_params=pltpu.CompilerParams(collective_id=1, has_side_effects=True),
    )(acc, stat, out_weight)


def shards(queries, lookup_sheets, content_sheets, page_table, context_len, out_weight):
    req_rows = page_table.shape[0]
    pool_local, page_len, kv_local, head_dim = lookup_sheets.shape
    span = page_len * kv_local
    all_queries, listed = gather_queries(
        queries, page_table.T, context_len.reshape(1, req_rows), (pool_local, page_len)
    )
    acc, stat = attend(
        listed.reshape(-1), all_queries.reshape(req_rows, *queries.shape[1:]),
        lookup_sheets.reshape(pool_local, span, head_dim),
        content_sheets.reshape(pool_local, span, head_dim), kv_local,
    )
    return finish(acc, stat, out_weight)


def solution(mesh):
    placed = (
        P("dp", "mp", None),
        P("dp", None, "mp", None),
        P("dp", None, "mp", None),
        P(),
        P(),
        P("mp", "dp"),
    )
    return jax.shard_map(
        shards,
        mesh=mesh,
        in_specs=placed,
        out_specs=(P("dp", "mp", None), P("mp", "dp")),
        check_vma=False,
    )
```

time: 248 us -> 172 us (0.69)
  Pallas kernels: 238 us -> 165 us
  other arithmetic: 3.33 us -> 0 us
    pallas_call x2, Pallas kernels: 109 us -> 69.4 us  [the longest x1 38.5 us: attend(): pl.pallas_call(functools.partial(attend_kernel, (kv_local, blocks)), out_...]
    pallas_call x1, Pallas kernels: 129 us -> 95.9 us  [finish(): pl.pallas_call(finish_kernel, out_shape=(jax.ShapeDtypeStruct((rows, q_lo...]
where the time goes in v2:
time: 172 us; the launch traced here: 169 us
  Pallas kernels  165 us (96%)
  local copies, waits for them, and re-layouts  3.14 us (2%)
    pallas_call x1, Pallas kernels, finish(): pl.pallas_call(finish_kernel, out_shape=(jax.ShapeDtypeStruct((rows, q_lo...  95.9 us
    pallas_call x1, Pallas kernels, attend(): pl.pallas_call(functools.partial(attend_kernel, (kv_local, blocks)), out_...  38.5 us
    pallas_call x1, Pallas kernels, gather_queries(): pl.pallas_call(functools.partial(gather_kernel, sizes), out_shape=(jax.Sh...  30.8 us

profile of v2, /device:TPU:4, one launch (start us, length us, event | category | flops | bytes accessed | tf_op | source)
XLA Modules:
  0.0 169.0 jit_solution(14879551299823640032)
XLA Ops:
  0.6 30.8 %shard_map.77 = (bf16[4,4,2,4,8,16,128]{6,5,4,3,2,1,0:T(8,128)(2,1)}, s32[24,128]{1,0:T(8,128)}) custom-call(bf16[4,8,16,128]{3,2,1,0:T(8,128)(2,1)} %bitcast.10, s32[32,1024]{1,0:T(8,128)} %bitcast.11, s32[1,1024]{1,0:T(1,128)} %bitcast.13), custom_call_target="tpu_custom_call" | custom-call | tf_op jit(solution)/shard_map/pallas_call | solution.py:205
  31.5 38.5 %shard_map.78 = (f32[33,32,16,128]{3,2,1,0:T(8,128)}, f32[33,2,16,128]{3,2,1,0:T(8,128)}) custom-call(s32[3072]{0:T(1024)} %bitcast.12, bf16[1024,16,128]{2,1,0:T(8,128)(2,1)} %bitcast.9, bf16[1024,32,128]{2,1,0:T(8,128)(2,1)} %bitcast.7, bf16[1024,32,128]{2,1,0:T(8,128)(2,1)} %bitcast.8), custom_call_target="tpu_custom_call" | custom-call | tf_op jit(solution)/shard_map/pallas_call | solution.py:312
  70.0 95.9 %shard_map.79 = (bf16[32,16,128]{2,1,0:T(8,128)(2,1)}, bf16[256,256]{1,0:T(8,128)(2,1)}) custom-call(f32[33,32,16,128]{3,2,1,0:T(8,128)} %get-tuple-element.8.acc_hbm, f32[33,2,16,128]{3,2,1,0:T(8,128)} %get-tuple-element.9.stat_hbm, bf16[2048,256]{1,0:T(8,128)(2,1)} %w_hbm.1), custom_call_target="tpu_custom_call" | custom-call | tf_op jit(solution)/shard_map/pallas_call | solution.py:577
  165.9 1.6 copy.10
  167.5 1.6 copy.11
